TPU v7x, 32 devices: a whole 2x2x4 slice. The times are simulated.
32 devices in a mesh: rep: 32 (over z, y, x, core).
Axes of the slice: x: 2, y: 2, z: 4, core: 2. Of those that a mesh axis runs over, the one named last changes fastest.
Arguments:
- inputs: bfloat16 [16384, 1024], P('rep'), may hold values from -6 to 6
- out_grads: bfloat16 [16384, 4096], P('rep'), may hold values from -0.29882812 to 0.29882812
- error_in: bfloat16 [32, 1024, 4096], P('rep'), may hold values from -6 to 6
- q_start: float32 [32, 4096], replicated, may hold values from -0.09375 to 0.09375
- master: float32 [1024, 4096], P(None, 'rep'), may hold values from -1.2 to 1.2
Outputs:
- error_out: bfloat16 [32, 1024, 4096], P('rep')
- q_out: float32 [32, 4096], replicated
- master_out: float32 [1024, 4096], P(None, 'rep')
All inputs are finite; a program needn't handle non-finite values.
Results may differ from a plain program's by a relative error of at most 0.001.
Values sent between devices are 32-bit elements; how exact they have to be, the bound alone decides.
No kernel may reach another device: no remote copies, remote signals or barrier semaphores. Data moves between devices by JAX's collectives and lax.ppermute only.
A program may use at most 128 MiB of HBM per device.

v0:
```python
import jax
import jax.numpy as jnp
from jax import lax
from jax.sharding import PartitionSpec as P

ITERS = 3


def orthonormal(rows):
    basis = jnp.zeros_like(rows)
    for k in range(rows.shape[0]):
        vector = rows[k]
        coef = jnp.dot(basis, vector, precision=lax.Precision.HIGHEST)
        vector = vector - jnp.dot(coef, basis, precision=lax.Precision.HIGHEST)
        basis = basis.at[k].set(vector / jnp.sqrt(jnp.sum(vector * vector) + 1.0))
    return basis


def outer_rows(left, right):
    return lax.dot_general(
        left,
        right,
        (((0,), (0,)), ((), ())),
        precision=lax.Precision.HIGHEST,
        preferred_element_type=jnp.float32,
    )


def shards(inputs, out_grads, error_in, q_start, master):
    count = lax.axis_size("rep")
    grad = lax.dot_general(
        inputs, out_grads, (((0,), (0,)), ((), ())), preferred_element_type=jnp.float32
    )
    merged = grad + error_in[0].astype(jnp.float32)
    factor = q_start
    basis = None
    local_q = None
    for step in range(ITERS):
        local_p = lax.dot_general(
            factor,
            merged,
            (((1,), (1,)), ((), ())),
            precision=lax.Precision.HIGHEST,
            preferred_element_type=jnp.float32,
        )
        total_p = lax.psum(local_p, "rep")
        basis = orthonormal(total_p)
        local_q = jnp.dot(
            basis, merged, precision=lax.Precision.HIGHEST, preferred_element_type=jnp.float32
        )
        if step + 1 < ITERS:
            factor = lax.psum(local_q, "rep") / count
    width = master.shape[1]
    factor = lax.psum(local_q, "rep") / count
    recon = outer_rows(basis, factor)
    own_cols = lax.dynamic_slice_in_dim(recon, lax.axis_index("rep") * width, width, 1)
    master_out = master - 0.5 * own_cols
    error_out = (merged - recon).astype(jnp.bfloat16)[None]
    return (error_out, factor, master_out)


def solution(mesh):
    return jax.shard_map(
        shards,
        mesh=mesh,
        in_specs=(P("rep", None), P("rep", None), P("rep", None, None), P(), P(None, "rep")),
        out_specs=(P("rep", None, None), P(), P(None, "rep")),
        check_vma=False,
    )
```

profile of v0, /device:TPU:0, one launch (start us, length us, event | category | flops | bytes accessed | tf_op | source)
XLA Modules:
  0.0 1167.3 jit_solution(7776026956208568537)
XLA Ops:
  7.2 1.2 copy-done
  8.4 8.8 convert_add_fusion
  17.2 5.7 copy-done.1
  22.9 16.0 %convolution_bitcast_fusion = f32[32,1024]{1,0:T(8,128)} fusion(f32[1024,4096]{1,0:T(8,128)S(1)} %convert_add_fusion, f32[32,4096]{1,0:T(8,128)S(1)} %copy-done.3), kind=kOutput, calls=%fused_computation.3 | convolution fusion | flops 1610612736 | bytes 17432576 | tf_op jit(solution)/shard_map/dot_general | solution.py:39
  39.1 127.2 %all-reduce.10.cloned.1.call-done = f32[32,1024]{1,0:T(8,128)} async-done(((f32[32,1024]{1,0:T(8,128)}), f32[32,1024]{1,0:T(8,128)}) %all-reduce.10.cloned.1.call-update) | async-done | bytes 131088 | tf_op jit(solution)/shard_map/psum | solution.py:46
  167.4 1.2 fusion.236
  172.4 0.9 convolution_bitcast_fusion.94
  175.0 0.9 convolution_bitcast_fusion.93
  180.2 0.9 convolution_bitcast_fusion.91
  185.4 0.9 convolution_bitcast_fusion.89
  190.5 0.9 convolution_bitcast_fusion.87
  195.7 0.9 convolution_bitcast_fusion.85
  198.3 0.9 convolution_bitcast_fusion.84
  200.9 0.9 convolution_bitcast_fusion.83
  202.1 1.3 fusion.235
  251.6 13.9 %fusion.267 = f32[32,4096]{1,0:T(8,128)} fusion(f32[32,1024]{1,0:T(8,128)S(1)} %scatter.371, f32[1024,4096]{1,0:T(8,128)} %copy-done.1), kind=kOutput, calls=%fused_computation.560 | convolution fusion | flops 1610612736 | bytes 17432576 | tf_op jit(solution)/shard_map/dot_general | solution.py:48
  265.6 128.2 %all-reduce.12.cloned.1.call-done = f32[32,4096]{1,0:T(8,128)} async-done(((f32[32,4096]{1,0:T(8,128)}), f32[32,4096]{1,0:T(8,128)}) %all-reduce.12.cloned.1.call-update) | async-done | bytes 524304 | tf_op jit(solution)/shard_map/psum | solution.py:52
  393.8 19.3 %fusion.3 = f32[32,1024]{1,0:T(8,128)} fusion(f32[1024,4096]{1,0:T(8,128)} %copy-done.1, f32[32,4096]{1,0:T(8,128)} %all-reduce.12.cloned.1.call-done), kind=kOutput, calls=%fused_computation.103 | convolution fusion | flops 1610743808 | bytes 17432576 | tf_op jit(solution)/shard_map/dot_general | solution.py:39
  413.2 123.6 %all-reduce.14.cloned.1.call-done = f32[32,1024]{1,0:T(8,128)} async-done(((f32[32,1024]{1,0:T(8,128)}), f32[32,1024]{1,0:T(8,128)}) %all-reduce.14.cloned.1.call-update) | async-done | bytes 131088 | tf_op jit(solution)/shard_map/psum | solution.py:46
  537.9 1.2 fusion.234
  573.0 1.3 fusion.233
  622.4 13.9 %fusion.298 = f32[32,4096]{1,0:T(8,128)} fusion(f32[32,1024]{1,0:T(8,128)S(1)} %scatter.425, f32[1024,4096]{1,0:T(8,128)} %copy-done.1), kind=kOutput, calls=%fused_computation.591 | convolution fusion | flops 1610612736 | bytes 17432576 | tf_op jit(solution)/shard_map/dot_general | solution.py:48
  636.5 128.1 %all-reduce.16.cloned.1.call-done = f32[32,4096]{1,0:T(8,128)} async-done(((f32[32,4096]{1,0:T(8,128)}), f32[32,4096]{1,0:T(8,128)}) %all-reduce.16.cloned.1.call-update) | async-done | bytes 524304 | tf_op jit(solution)/shard_map/psum | solution.py:52
  764.6 19.3 %fusion.1 = f32[32,1024]{1,0:T(8,128)} fusion(f32[1024,4096]{1,0:T(8,128)} %copy-done.1, f32[32,4096]{1,0:T(8,128)} %all-reduce.16.cloned.1.call-done), kind=kOutput, calls=%fused_computation.101 | convolution fusion | flops 1610743808 | bytes 17432576 | tf_op jit(solution)/shard_map/dot_general | solution.py:39
  784.0 123.6 %all-reduce.18.cloned.1.call-done = f32[32,1024]{1,0:T(8,128)} async-done(((f32[32,1024]{1,0:T(8,128)}), f32[32,1024]{1,0:T(8,128)}) %all-reduce.18.cloned.1.call-update) | async-done | bytes 131088 | tf_op jit(solution)/shard_map/psum | solution.py:46
  908.6 1.2 fusion.232
  943.3 1.3 fusion.231
  992.7 14.1 %fusion.329 = f32[32,4096]{1,0:T(8,128)} fusion(f32[32,1024]{1,0:T(8,128)S(1)} %scatter.479, f32[1024,4096]{1,0:T(8,128)} %copy-done.1), kind=kOutput, calls=%fused_computation.622 | convolution fusion | flops 1610612736 | bytes 17432576 | tf_op jit(solution)/shard_map/dot_general | solution.py:48
  1006.8 128.3 %all-reduce.20.cloned.1.call-done = f32[32,4096]{1,0:T(8,128)} async-done(((f32[32,4096]{1,0:T(8,128)}), f32[32,4096]{1,0:T(8,128)}) %all-reduce.20.cloned.1.call-update) | async-done | bytes 524304 | tf_op jit(solution)/shard_map/psum | solution.py:54
  1135.0 1.1 broadcast_multiply_fusion
  1136.1 13.6 %fusion.330 = f32[1024,4096]{1,0:T(8,128)S(1)} fusion(f32[32,1024]{1,0:T(8,128)S(1)} %scatter.479, f32[32,4096]{1,0:T(8,128)S(1)} %broadcast_multiply_fusion), kind=kOutput, calls=%fused_computation.623 | convolution fusion | flops 1610612736 | bytes 17432576 | tf_op jit(solution)/shard_map/dot_general | solution.py:20
  1149.7 9.6 fusion
  (493 shorter events, 173.8 us)
Async XLA Ops:
  7.2 1.2 copy-start
  7.2 15.7 %copy-start.3 = (f32[32,4096]{1,0:T(8,128)S(1)}, f32[32,4096]{1,0:T(8,128)}, u32[]{:S(2)}) copy-start(f32[32,4096]{1,0:T(8,128)} %param.200) | copy-start | bytes 1572868
  7.2 159.1 %all-reduce.10.cloned.1.call-start = ((), (), s32[]{:S(2)}) async-start(), calls=%async_computation | async-start | bytes 262144 | tf_op jit(solution)/shard_map/psum | solution.py:46
  17.2 5.7 copy-start.1
  38.9 354.9 %all-reduce.12.cloned.1.call-start = ((), (), s32[]{:S(2)}) async-start(), calls=%async_computation.1 | async-start | bytes 1048576 | tf_op jit(solution)/shard_map/psum | solution.py:52
  265.5 271.2 %all-reduce.14.cloned.1.call-start = ((), (), s32[]{:S(2)}) async-start(), calls=%async_computation.2 | async-start | bytes 262144 | tf_op jit(solution)/shard_map/psum | solution.py:46
  413.1 351.5 %all-reduce.16.cloned.1.call-start = ((), (), s32[]{:S(2)}) async-start(), calls=%async_computation.3 | async-start | bytes 1048576 | tf_op jit(solution)/shard_map/psum | solution.py:52
  636.3 271.2 %all-reduce.18.cloned.1.call-start = ((), (), s32[]{:S(2)}) async-start(), calls=%async_computation.4 | async-start | bytes 262144 | tf_op jit(solution)/shard_map/psum | solution.py:46
  783.9 351.1 %all-reduce.20.cloned.1.call-start = ((), (), s32[]{:S(2)}) async-start(), calls=%async_computation.5 | async-start | bytes 1048576 | tf_op jit(solution)/shard_map/psum | solution.py:54
  1136.1 23.2 %copy-start.2 = (f32[32,4096]{1,0:T(8,128)}, f32[32,4096]{1,0:T(8,128)S(1)}, u32[]{:S(2)}) copy-start(f32[32,4096]{1,0:T(8,128)S(1)} %broadcast_multiply_fusion) | copy-start | bytes 1572868
  1149.7 9.6 copy-start.4
Sparse Core Ops, SparseCore 0:
  39.0 127.2 all-reduce.9
  265.7 128.1 all-reduce.11
  413.3 123.4 all-reduce.13
  636.4 128.1 all-reduce.15
  784.0 123.4 all-reduce.17
  1006.9 128.0 all-reduce.19
where the time goes:
time: 1180 us; the launch traced here: 1170 us
  waiting for transfers between devices  759 us (64%)
  matrix products  229 us (19%)
  between operations  83.2 us (7%)
  other arithmetic  69.8 us (6%)
  local copies, waits for them, and re-layouts  25.2 us (2%)
    psum x3, waiting for transfers between devices, shards(): factor = lax.psum(local_q, 'rep') / count  385 us
    psum x3, waiting for transfers between devices, shards(): total_p = lax.psum(local_p, 'rep')  374 us
    dot_general x96, matrix products, orthonormal(): coef = jnp.dot(basis, vector, precision=lax.Precision.HIGHEST)  89.7 us
    reduce_sum x96, other arithmetic, orthonormal(): basis = basis.at[k].set(vector / jnp.sqrt(jnp.sum(vector * vector) + 1.0))  57.8 us
    dot_general x3, matrix products, shards(): lax.dot_general(factor, merged, (((1,), (1,)), ((), ())), precision=lax.P...  54.5 us
    dot_general x3, matrix products, shards(): jnp.dot(basis, merged, precision=lax.Precision.HIGHEST, preferred_element...  41.9 us
  transfers between devices with their start and end apart: 6, of which 6 were waited for; matrix products, arithmetic and copies ran while one was open for 0% of the time, Pallas kernels for 0%

commit v1 on v0

--- a/solution.py
+++ b/solution.py
@@ -43,7 +43,11 @@
             precision=lax.Precision.HIGHEST,
             preferred_element_type=jnp.float32,
         )
-        total_p = lax.psum(local_p, "rep")
+        total_p = local_p
+        for hop in (1, 2, 4, 8, 16):
+            total_p = total_p + lax.ppermute(
+                total_p, "rep", [(dev, dev ^ hop) for dev in range(32)]
+            )
         basis = orthonormal(total_p)
         local_q = jnp.dot(
             basis, merged, precision=lax.Precision.HIGHEST, preferred_element_type=jnp.float32

time: 1180 us -> 866 us (0.73)
  waiting for transfers between devices: 759 us -> 439 us
  starting transfers between devices: 0.59 us -> 23.4 us
    psum x3 -> x0, waiting for transfers between devices: 374 us -> none  [shards(): total_p = lax.psum(local_p, 'rep')]
    ppermute x0 -> x15, waiting for transfers between devices: none -> 51.9 us  [shards(): lax.ppermute(total_p, 'rep', [(dev, dev ^ hop) for dev in range(32)])]
    ppermute x0 -> x15, starting transfers between devices: none -> 23.1 us  [shards(): lax.ppermute(total_p, 'rep', [(dev, dev ^ hop) for dev in range(32)])]
  transfers between devices with their start and end apart: 6 -> 18, of which waited for: 6 -> 18; matrix products, arithmetic and copies ran while one was open for 0% -> 0% of each run, Pallas kernels for 0% -> 0%
where the time goes in v1:
time: 866 us; the launch traced here: 856 us
  waiting for transfers between devices  439 us (51%)
  matrix products  223 us (26%)
  between operations  83 us (10%)
  other arithmetic  70.1 us (8%)
  starting transfers between devices  23.4 us (3%)
  local copies, waits for them, and re-layouts  18 us (2%)
    psum x3, waiting for transfers between devices, shards(): factor = lax.psum(local_q, 'rep') / count  387 us
    dot_general x96, matrix products, orthonormal(): coef = jnp.dot(basis, vector, precision=lax.Precision.HIGHEST)  85.3 us
    reduce_sum x96, other arithmetic, orthonormal(): basis = basis.at[k].set(vector / jnp.sqrt(jnp.sum(vector * vector) + 1.0))  57.8 us
    dot_general x3, matrix products, shards(): lax.dot_general(factor, merged, (((1,), (1,)), ((), ())), precision=lax.P...  52.7 us
    ppermute x15, waiting for transfers between devices, shards(): lax.ppermute(total_p, 'rep', [(dev, dev ^ hop) for dev in range(32)])  51.9 us
    dot_general x3, matrix products, shards(): jnp.dot(basis, merged, precision=lax.Precision.HIGHEST, preferred_element...  41.9 us
    ppermute x15, starting transfers between devices, shards(): lax.ppermute(total_p, 'rep', [(dev, dev ^ hop) for dev in range(32)])  23.1 us
    dot_general x96, matrix products, orthonormal(): vector = vector - jnp.dot(coef, basis, precision=lax.Precision.HIGHEST)  20.9 us
  transfers between devices with their start and end apart: 18, of which 18 were waited for; matrix products, arithmetic and copies ran while one was open for 0% of the time, Pallas kernels for 0%

profile of v1, /device:TPU:0, one launch (start us, length us, event | category | flops | bytes accessed | tf_op | source)
XLA Modules:
  0.0 856.2 jit_solution(14471267732066899633)
XLA Ops:
  8.4 8.8 %convert_add_fusion = f32[1024,4096]{1,0:T(8,128)S(1)} fusion(bf16[1,1024,4096]{2,1,0:T(8,128)(2,1)} %param.199, bf16[512,1024]{1,0:T(8,128)(2,1)S(1)} %copy-done, bf16[512,4096]{1,0:T(8,128)(2,1)} %param.198), kind=kOutput, calls=%fused_computation | convolution fusion | flops 4303355904 | bytes 30408704 | tf_op jit(solution)/shard_map/dot_general | solution.py:31
  17.2 5.7 copy-done.2
  22.9 15.3 %convolution_bitcast_fusion = f32[32,1024]{1,0:T(8,128)S(1)} fusion(f32[1024,4096]{1,0:T(8,128)S(1)} %convert_add_fusion, f32[32,4096]{1,0:T(8,128)S(1)} %copy-done.7), kind=kOutput, calls=%fused_computation.3 | convolution fusion | flops 1610612736 | bytes 17432576 | tf_op jit(solution)/shard_map/dot_general | solution.py:39
  39.8 3.1 collective-permute-start.1
  42.8 3.8 collective-permute-done.1
  46.7 1.8 collective-permute-start.2
  48.5 3.2 collective-permute-done.2
  51.7 1.9 collective-permute-start.3
  53.6 3.1 collective-permute-done.3
  56.8 3.3 collective-permute-start.4
  60.1 4.4 collective-permute-done.4
  145.8 14.1 %fusion.267 = f32[32,4096]{1,0:T(8,128)} fusion(f32[32,1024]{1,0:T(8,128)S(1)} %scatter.371, f32[1024,4096]{1,0:T(8,128)} %copy-done.2), kind=kOutput, calls=%fused_computation.560 | convolution fusion | flops 1610612736 | bytes 17432576 | tf_op jit(solution)/shard_map/dot_general | solution.py:52
  160.0 130.3 %all-reduce.7.cloned.1.call-done = f32[32,4096]{1,0:T(8,128)} async-done(((f32[32,4096]{1,0:T(8,128)}), f32[32,4096]{1,0:T(8,128)}) %all-reduce.7.cloned.1.call-update) | async-done | bytes 524304 | tf_op jit(solution)/shard_map/psum | solution.py:56
  290.3 18.7 %fusion.3 = f32[32,1024]{1,0:T(8,128)S(1)} fusion(f32[1024,4096]{1,0:T(8,128)} %copy-done.2, f32[32,4096]{1,0:T(8,128)} %all-reduce.7.cloned.1.call-done), kind=kOutput, calls=%fused_computation.103 | convolution fusion | flops 1610743808 | bytes 17432576 | tf_op jit(solution)/shard_map/dot_general | solution.py:39
  311.9 4.1 collective-permute-done.6
  316.0 1.5 collective-permute-start.7
  317.6 3.5 collective-permute-done.7
  322.6 3.5 collective-permute-done.8
  327.6 5.8 collective-permute-done.9
  415.2 13.9 %fusion.298 = f32[32,4096]{1,0:T(8,128)} fusion(f32[32,1024]{1,0:T(8,128)S(1)} %scatter.425, f32[1024,4096]{1,0:T(8,128)} %copy-done.2), kind=kOutput, calls=%fused_computation.591 | convolution fusion | flops 1610612736 | bytes 17432576 | tf_op jit(solution)/shard_map/dot_general | solution.py:52
  429.3 128.1 %all-reduce.9.cloned.1.call-done = f32[32,4096]{1,0:T(8,128)} async-done(((f32[32,4096]{1,0:T(8,128)}), f32[32,4096]{1,0:T(8,128)}) %all-reduce.9.cloned.1.call-update) | async-done | bytes 524304 | tf_op jit(solution)/shard_map/psum | solution.py:56
  557.4 18.7 %fusion.1 = f32[32,1024]{1,0:T(8,128)S(1)} fusion(f32[1024,4096]{1,0:T(8,128)} %copy-done.2, f32[32,4096]{1,0:T(8,128)} %all-reduce.9.cloned.1.call-done), kind=kOutput, calls=%fused_computation.101 | convolution fusion | flops 1610743808 | bytes 17432576 | tf_op jit(solution)/shard_map/dot_general | solution.py:39
  579.0 4.1 collective-permute-done.11
  583.1 1.5 collective-permute-start.12
  584.7 3.5 collective-permute-done.12
  588.2 1.5 collective-permute-start.13
  589.7 3.5 collective-permute-done.13
  594.8 5.8 collective-permute-done.14
  682.1 13.9 %fusion.329 = f32[32,4096]{1,0:T(8,128)} fusion(f32[32,1024]{1,0:T(8,128)S(1)} %scatter.479, f32[1024,4096]{1,0:T(8,128)} %copy-done.2), kind=kOutput, calls=%fused_computation.622 | convolution fusion | flops 1610612736 | bytes 17432576 | tf_op jit(solution)/shard_map/dot_general | solution.py:52
  696.0 128.2 %all-reduce.11.cloned.1.call-done = f32[32,4096]{1,0:T(8,128)} async-done(((f32[32,4096]{1,0:T(8,128)}), f32[32,4096]{1,0:T(8,128)}) %all-reduce.11.cloned.1.call-update) | async-done | bytes 524304 | tf_op jit(solution)/shard_map/psum | solution.py:58
  825.4 13.6 %fusion.330 = f32[1024,4096]{1,0:T(8,128)S(1)} fusion(f32[32,1024]{1,0:T(8,128)S(1)} %scatter.479, f32[32,4096]{1,0:T(8,128)S(1)} %broadcast_multiply_fusion), kind=kOutput, calls=%fused_computation.623 | convolution fusion | flops 1610612736 | bytes 17432576 | tf_op jit(solution)/shard_map/dot_general | solution.py:20
  839.0 9.6 %fusion = bf16[1,1024,4096]{2,1,0:T(8,128)(2,1)} fusion(f32[1024,4096]{1,0:T(8,128)} %copy-done.2, f32[1024,4096]{1,0:T(8,128)S(1)} %fusion.330), kind=kLoop, calls=%fused_computation.2 | loop fusion | flops 8388608 | bytes 41943040 | tf_op jit(solution)/shard_map/broadcast_in_dim | solution.py:62
  (537 shorter events, 191.3 us)
Async XLA Ops:
  7.2 1.2 copy-start
  7.2 15.7 %copy-start.7 = (f32[32,4096]{1,0:T(8,128)S(1)}, f32[32,4096]{1,0:T(8,128)}, u32[]{:S(2)}) copy-start(f32[32,4096]{1,0:T(8,128)} %param.200) | copy-start | bytes 1572868
  7.2 283.1 %all-reduce.7.cloned.1.call-start = ((), (), s32[]{:S(2)}) async-start(), calls=%async_computation | async-start | bytes 1048576 | tf_op jit(solution)/shard_map/psum | solution.py:56
  17.2 5.7 copy-start.2
  38.2 1.5 collective-permute-start
  39.8 6.9 collective-permute-start.1
  46.7 5.0 collective-permute-start.2
  51.7 5.0 collective-permute-start.3
  56.8 7.7 collective-permute-start.4
  64.5 3.6 copy-start.4
  159.9 397.4 %all-reduce.9.cloned.1.call-start = ((), (), s32[]{:S(2)}) async-start(), calls=%async_computation.1 | async-start | bytes 1048576 | tf_op jit(solution)/shard_map/psum | solution.py:56
  308.9 1.4 collective-permute-start.5
  310.4 5.6 collective-permute-start.6
  316.0 5.0 collective-permute-start.7
  321.1 5.0 collective-permute-start.8
  326.1 7.3 collective-permute-start.9
  333.5 3.6 copy-start.5
  429.1 395.2 %all-reduce.11.cloned.1.call-start = ((), (), s32[]{:S(2)}) async-start(), calls=%async_computation.2 | async-start | bytes 1048576 | tf_op jit(solution)/shard_map/psum | solution.py:58
  576.1 1.4 collective-permute-start.10
  577.5 5.6 collective-permute-start.11
  583.1 5.0 collective-permute-start.12
  588.2 5.0 collective-permute-start.13
  593.2 7.3 collective-permute-start.14
  600.6 3.6 copy-start.3
  825.3 23.2 %copy-start.6 = (f32[32,4096]{1,0:T(8,128)}, f32[32,4096]{1,0:T(8,128)S(1)}, u32[]{:S(2)}) copy-start(f32[32,4096]{1,0:T(8,128)S(1)} %broadcast_multiply_fusion) | copy-start | bytes 1572868
  825.4 24.1 %copy-start.1 = (bf16[512,1024]{1,0:T(8,128)(2,1)S(1)}, bf16[512,1024]{1,0:T(8,128)(2,1)}, u32[]{:S(2)}) copy-start(bf16[512,1024]{1,0:T(8,128)(2,1)} %param.197) | copy-start | bytes 3145732
  839.0 9.6 %copy-start.8 = (f32[1024,128]{1,0:T(8,128)S(1)}, f32[1024,128]{1,0:T(8,128)}, u32[]{:S(2)}) copy-start(f32[1024,128]{1,0:T(8,128)} %param.201) | copy-start | bytes 1572868
Sparse Core Ops, SparseCore 0:
  160.0 130.1 all-reduce.6
  429.2 128.1 all-reduce.8
  696.1 128.0 all-reduce.10
